TPU v7x, 128 devices: a whole 4x4x4 slice. The times are simulated.
128 devices in a mesh: scen: 32 (over z, y_lo, x), fac: 4 (over y_hi, core).
Axes of the slice: x: 4, y: 4 (y_hi: 2, y_lo: 2; y = y_hi * 2 + y_lo), z: 4, core: 2. Of those that a mesh axis runs over, the one named last changes fastest.
Arguments:
- scenario_draws: bfloat16 [32768, 4096], P('scen'), may hold values from -6 to 6
- cholesky: bfloat16 [4096, 4096], P('scen', 'fac'), may hold values from -1.5 to 1.5, as said below
- exposures: bfloat16 [4096, 4096], P('fac'), may hold values from -0.09375 to 0.09375
- drift: float32 [4096], P('fac'), may hold values from -3 to 3
Outputs:
- covariance: float32 [4096, 4096], P('scen', 'fac')
- expected: float32 [4096], P('fac')
Inputs may be any that keep to these rules, and one draw needn't show every extreme that they name: cholesky is lower triangular (zero above the diagonal) with diagonal entries of 0.5 to 1.5.
All inputs are finite; a program needn't handle non-finite values.
Results may differ from a plain program's by a relative error of at most 0.0013.
Values may be sent and summed in bfloat16 or wider, within the bound.
No kernel may reach another device: no remote copies, remote signals or barrier semaphores. Data moves between devices by JAX's collectives and lax.ppermute only.
A program may use at most 128 MiB of HBM per device.

v0:
```python
import jax
import jax.numpy as jnp
from jax import lax
from jax.sharding import Mesh
from jax.sharding import PartitionSpec as P

SCEN = ("scen_0", "scen_1", "scen_2")


def in_order(tiles, dim):
    tiles = jnp.moveaxis(tiles, 0, dim)
    shape = tiles.shape
    return tiles.reshape(*shape[:dim], shape[dim] * shape[dim + 1], *shape[dim + 2 :])


def gather_in_order(x, axes, order):
    tiles = x
    for k in order:
        tiles = lax.all_gather(tiles, axes[k])
    done = order[::-1]
    back = [done.index(k) for k in range(len(axes))]
    tiles = tiles.transpose(*back, *range(len(axes), tiles.ndim))
    return tiles.reshape(-1, *x.shape)


def whole_of(x, axes, order, dim):
    return in_order(gather_in_order(x, axes, order), dim)


def from_everyone(x, axis):
    copies = jnp.broadcast_to(x, (lax.axis_size(axis), *x.shape))
    return lax.all_to_all(copies, axis, split_axis=0, concat_axis=0, tiled=True)


def over_copies(x, axis):
    return from_everyone(x, axis).sum(axis=0)


def on_device(scenario_draws, cholesky, exposures, drift):
    count_rows = scenario_draws.shape[0]
    own_desks = exposures.shape[0]
    mixed = jnp.dot(
        scenario_draws, whole_of(cholesky, SCEN, (1, 0, 2), 0), preferred_element_type=jnp.float32
    )
    shocks = (mixed + drift[None, :]).astype(jnp.bfloat16)
    pnl_acc = lax.dot_general(
        lax.all_gather(shocks, "fac", axis=1, tiled=True),
        exposures,
        (((1,), (1,)), ((), ())),
        preferred_element_type=jnp.float32,
    )
    pnl = pnl_acc.astype(jnp.bfloat16)
    gathered = lax.all_gather(pnl, "fac", axis=1, tiled=True)
    desk_total = gathered.shape[1]
    column_sums = over_copies(jnp.sum(gathered, axis=0, dtype=jnp.float32), SCEN)
    scenario_total = count_rows * lax.axis_size(SCEN)
    means = column_sums / scenario_total
    col_means = lax.dynamic_slice_in_dim(means, lax.axis_index("fac") * own_desks, own_desks, 0)
    owned_rows = desk_total // lax.axis_size(SCEN)
    row_start = lax.axis_index(SCEN) * owned_rows
    block = lax.psum_scatter(
        lax.dot_general(
            gathered, pnl, (((0,), (0,)), ((), ())), preferred_element_type=jnp.float32
        ),
        SCEN,
        scatter_dimension=0,
        tiled=True,
    )
    row_means = lax.dynamic_slice_in_dim(means, row_start, owned_rows, 0)
    covariance = (block - scenario_total * row_means[:, None] * col_means[None, :]) / (
        scenario_total - 1
    )
    return (covariance, col_means)


def solution(mesh):
    torus = Mesh(
        mesh.devices.reshape(4, 2, 4, mesh.shape["fac"]), ("scen_0", "scen_1", "scen_2", "fac")
    )
    in_specs = (P(SCEN, None), P(SCEN, "fac"), P("fac", None), P("fac"))
    out_specs = (P(SCEN, "fac"), P("fac"))
    return jax.shard_map(
        on_device, mesh=torus, in_specs=in_specs, out_specs=out_specs, check_vma=False
    )
```

profile of v0, /device:TPU:0, one launch (start us, length us, event | category | flops | bytes accessed | tf_op | source)
XLA Modules:
  0.0 532.6 jit_solution(352595188754719642)
XLA Ops:
  7.2 0.0 all-gather.12.cloned.1.call-start
  7.2 10.6 %all-gather = bf16[256,1024]{1,0:T(8,128)(2,1)} all-gather(bf16[128,1024]{1,0:T(8,128)(2,1)} %param.5), channel_id=2, replica_groups=mesh['scen_0'=4,'scen_1'=2,'scen_2'=4,'fac'=4] {'scen_1'}, dimensions={0}, use_global_device_ids=true | all-gather | bytes 786432 | tf_op jit(solution)/shard_map/all_gather | solution.py:19
  17.8 0.0 all-gather.12.cloned.1.call-update
  17.9 0.0 all-gather.14.cloned.1.call-start
  17.9 33.2 %all-gather.12.cloned.1.call-done = bf16[8,128,1024]{2,1,0:T(8,128)(2,1)} async-done(((bf16[2,128,1024]{2,1,0:T(8,128)(2,1)}), bf16[8,128,1024]{2,1,0:T(8,128)(2,1)}) %all-gather.12.cloned.1.call-update) | async-done | bytes 2097168 | tf_op jit(solution)/shard_map/all_gather | solution.py:19
  51.1 0.0 all-gather.14.cloned.1.call-update
  51.1 0.0 all-gather.8.cloned.1.call-start
  51.2 84.5 %all-gather.14.cloned.1.call-done = bf16[16,2,128,1024]{3,2,1,0:T(8,128)(2,1)} async-done(((bf16[4,2,128,1024]{3,2,1,0:T(8,128)(2,1)}), bf16[16,2,128,1024]{3,2,1,0:T(8,128)(2,1)}) %all-gather.14.cloned.1.call-update) | async-done | bytes 8388624 | tf_op jit(solution)/shard_map/all_gather | solution.py:19
  135.7 0.0 copy-start.1
  135.7 8.2 %copy.9 = bf16[4,2,4,128,1024]{4,3,2,1,0:T(8,128)(2,1)} copy(bf16[4,2,4,128,1024]{4,3,1,0,2:T(8,128)(2,1)} %bitcast.12) | data formatting | bytes 16777216 | tf_op jit(solution)/shard_map/transpose | solution.py:22
  143.9 0.0 copy-done.1
  143.9 14.7 %add_convert_fusion = bf16[1024,1024]{1,0:T(8,128)(2,1)} fusion(f32[1024]{0:T(1024)S(1)} %copy-done.1, bf16[1024,4096]{1,0:T(8,128)(2,1)} %param.4, bf16[4096,1024]{1,0:T(8,128)(2,1)} %bitcast.13), kind=kOutput, calls=%fused_computation.1 | convolution fusion | flops 8592031744 | bytes 18878464 | tf_op jit(solution)/shard_map/dot_general | solution.py:42
  158.6 0.0 all-gather.8.cloned.1.call-update
  158.7 0.0 all-gather.10.cloned.1.call-start
  158.7 63.4 %all-gather.8.cloned.1.call-done = bf16[1024,4096]{1,0:T(8,128)(2,1)} async-done(((bf16[1024,1024]{1,0:T(8,128)(2,1)}), bf16[1024,4096]{1,0:T(8,128)(2,1)}) %all-gather.8.cloned.1.call-update) | async-done | bytes 8388624 | tf_op jit(solution)/shard_map/all_gather | solution.py:47
  222.1 14.8 %convolution_convert_fusion = bf16[1024,1024]{1,0:T(8,128)(2,1)} fusion(bf16[1024,4096]{1,0:T(8,128)(2,1)} %all-gather.8.cloned.1.call-done, bf16[1024,4096]{1,0:T(8,128)(2,1)} %param.6), kind=kOutput, calls=%fused_computation.2 | convolution fusion | flops 8590983168 | bytes 18874368 | tf_op jit(solution)/shard_map/dot_general | solution.py:46
  236.9 0.0 all-gather.10.cloned.1.call-update
  236.9 0.2 reduce-scatter.2.cloned.1.call-start
  237.1 61.6 %all-gather.10.cloned.1.call-done = bf16[1024,4096]{1,0:T(8,128)(2,1)} async-done(((bf16[1024,1024]{1,0:T(8,128)(2,1)}), bf16[1024,4096]{1,0:T(8,128)(2,1)}) %all-gather.10.cloned.1.call-update) | async-done | bytes 8388624 | tf_op jit(solution)/shard_map/all_gather | solution.py:53
  298.8 16.1 %fusion = f32[4096,1024]{1,0:T(8,128)} fusion(bf16[1024,4096]{1,0:T(8,128)(2,1)} %all-gather.10.cloned.1.call-done, bf16[1024,1024]{1,0:T(8,128)(2,1)} %convolution_convert_fusion), kind=kOutput, calls=%fused_computation.6 | convolution fusion | flops 8589934592 | bytes 27262976 | tf_op jit(solution)/shard_map/dot_general | solution.py:62
  314.9 0.0 reduce-scatter.2.cloned.1.call-update
  314.9 4.6 convert_reduce_fusion
  319.5 1.3 broadcast_in_dim.2
  320.7 7.3 %all-to-all-start = ((f32[32,1,4096]{2,1,0:T(1,128)}), f32[32,1,4096]{2,1,0:T(1,128)S(1)}, u32[]{:S(2)}, u32[]{:S(2)}) async-start(f32[32,1,4096]{2,1,0:T(1,128)} %broadcast_in_dim.2), calls=%async_computation.1 | async-start | bytes 1048576 | tf_op jit(solution)/shard_map/all_to_all | solution.py:32
  328.0 17.8 %all-to-all-done = f32[32,1,4096]{2,1,0:T(1,128)S(1)} async-done(((f32[32,1,4096]{2,1,0:T(1,128)}), f32[32,1,4096]{2,1,0:T(1,128)S(1)}, u32[]{:S(2)}, u32[]{:S(2)}) %all-to-all-start) | async-done | bytes 524320 | tf_op jit(solution)/shard_map/all_to_all | solution.py:32
  345.8 0.4 reduce_sum.19
  346.2 0.0 copy-start
  346.2 0.1 dynamic-slice_multiply_fusion
  346.3 177.8 %reduce-scatter.2.cloned.1.call-done = f32[128,1024]{1,0:T(8,128)} async-done(((f32[4096,1024]{1,0:T(8,128)}), f32[128,1024]{1,0:T(8,128)}) %reduce-scatter.2.cloned.1.call-update) | async-done | bytes 524304 | tf_op jit(solution)/shard_map/reduce_scatter | solution.py:61
  524.1 2.0 subtract_multiply_fusion
  526.0 0.0 copy-done
  (2 shorter events, 0.0 us)
Async XLA Ops:
  7.2 43.9 %all-gather.12.cloned.1.call-start = ((), (), s32[]{:S(2)}) async-start(), calls=%async_computation.5 | async-start | bytes 2621440 | tf_op jit(solution)/shard_map/all_gather | solution.py:19
  17.9 117.8 %all-gather.14.cloned.1.call-start = ((), (), s32[]{:S(2)}) async-start(), calls=%async_computation.6 | async-start | bytes 10485760 | tf_op jit(solution)/shard_map/all_gather | solution.py:19
  51.1 171.0 %all-gather.8.cloned.1.call-start = ((), (), s32[]{:S(2)}) async-start(), calls=%async_computation.2 | async-start | bytes 10485760 | tf_op jit(solution)/shard_map/all_gather | solution.py:47
  135.7 8.2 %copy-start.1 = (f32[1024]{0:T(1024)S(1)}, f32[1024]{0:T(1024)}, u32[]{:S(2)}) copy-start(f32[1024]{0:T(1024)} %param.7) | copy-start | bytes 12292
  158.7 140.1 %all-gather.10.cloned.1.call-start = ((), (), s32[]{:S(2)}) async-start(), calls=%async_computation.3 | async-start | bytes 10485760 | tf_op jit(solution)/shard_map/all_gather | solution.py:53
  236.9 287.2 %reduce-scatter.2.cloned.1.call-start = ((), (), s32[]{:S(2)}) async-start(), calls=%async_computation.4 | async-start | bytes 17301504 | tf_op jit(solution)/shard_map/reduce_scatter | solution.py:61
  320.7 25.1 %all-to-all-start = ((f32[32,1,4096]{2,1,0:T(1,128)}), f32[32,1,4096]{2,1,0:T(1,128)S(1)}, u32[]{:S(2)}, u32[]{:S(2)}) async-start(f32[32,1,4096]{2,1,0:T(1,128)} %broadcast_in_dim.2), calls=%async_computation.1 | async-start | bytes 1048576 | tf_op jit(solution)/shard_map/all_to_all | solution.py:32
  346.2 179.8 %copy-start = (f32[1024]{0:T(1024)}, f32[1024]{0:T(1024)S(1)}, u32[]{:S(2)}) copy-start(f32[1024]{0:T(1024)S(1)} %dynamic_slice.7) | copy-start | bytes 12292
Sparse Core Ops, SparseCore 0:
  18.0 33.0 all-gather.11
  52.8 82.8 all-gather.13
  158.8 63.2 all-gather.7
  237.0 61.6 all-gather.9
  315.0 209.0 reduce-scatter.1
where the time goes:
time: 533 us
  waiting for transfers between devices  438 us (82%)
  matrix products  45.6 us (9%)
  between operations  13.8 us (3%)
  blocking collectives  10.6 us (2%)
  local copies, waits for them, and re-layouts  9.51 us (2%)
  starting transfers between devices  7.64 us (1%)
  other arithmetic  6.96 us (1%)
    reduce_scatter x1, waiting for transfers between devices, on_device(): lax.psum_scatter(lax.dot_general(gathered, pnl, (((0,), (0,)), ((), ())),...  178 us
    all_gather x2, waiting for transfers between devices, gather_in_order(): tiles = lax.all_gather(tiles, axes[k])  118 us
    all_gather x1, waiting for transfers between devices, on_device(): lax.all_gather(shocks, 'fac', axis=1, tiled=True)  63.4 us
    all_gather x1, waiting for transfers between devices, on_device(): gathered = lax.all_gather(pnl, 'fac', axis=1, tiled=True)  61.6 us
    all_to_all x1, waiting for transfers between devices, from_everyone(): return lax.all_to_all(copies, axis, split_axis=0, concat_axis=0, tiled=True)  17.8 us
    dot_general x1, matrix products, on_device(): lax.dot_general(gathered, pnl, (((0,), (0,)), ((), ())), preferred_elemen...  16.1 us
    dot_general x1, matrix products, on_device(): lax.dot_general(lax.all_gather(shocks, 'fac', axis=1, tiled=True), exposu...  14.8 us
    dot_general x1, matrix products, on_device(): jnp.dot(scenario_draws, whole_of(cholesky, SCEN, (1, 0, 2), 0), preferred...  14.7 us
  transfers between devices with their start and end apart: 6, of which 6 were waited for; matrix products, arithmetic and copies ran while one was open for 1% of the time, Pallas kernels for 0%

commit v1 on v0

--- a/solution.py
+++ b/solution.py
@@ -50,7 +50,7 @@
         preferred_element_type=jnp.float32,
     )
     pnl = pnl_acc.astype(jnp.bfloat16)
-    gathered = lax.all_gather(pnl, "fac", axis=1, tiled=True)
+    gathered = jnp.concatenate(lax.all_gather(pnl, "fac"), axis=1)
     desk_total = gathered.shape[1]
     column_sums = over_copies(jnp.sum(gathered, axis=0, dtype=jnp.float32), SCEN)
     scenario_total = count_rows * lax.axis_size(SCEN)

time: 533 us -> 543 us (1.019)
  local copies, waits for them, and re-layouts: 9.51 us -> 21.1 us
    all_gather x0 -> x1, local copies, waits for them, and re-layouts: none -> 11.6 us  [on_device(): gathered = jnp.concatenate(lax.all_gather(pnl, 'fac'), axis=1)]
where the time goes in v1:
time: 543 us
  waiting for transfers between devices  439 us (81%)
  matrix products  43.9 us (8%)
  local copies, waits for them, and re-layouts  21.1 us (4%)
  between operations  13.8 us (3%)
  blocking collectives  10.6 us (2%)
  starting transfers between devices  7.63 us (1%)
  other arithmetic  6.95 us (1%)
    reduce_scatter x1, waiting for transfers between devices, on_device(): lax.psum_scatter(lax.dot_general(gathered, pnl, (((0,), (0,)), ((), ())),...  178 us
    all_gather x2, waiting for transfers between devices, gather_in_order(): tiles = lax.all_gather(tiles, axes[k])  118 us
    all_gather x1, waiting for transfers between devices, on_device(): lax.all_gather(shocks, 'fac', axis=1, tiled=True)  63.4 us
    all_gather x1, waiting for transfers between devices, on_device(): gathered = jnp.concatenate(lax.all_gather(pnl, 'fac'), axis=1)  61.6 us
    all_to_all x1, waiting for transfers between devices, from_everyone(): return lax.all_to_all(copies, axis, split_axis=0, concat_axis=0, tiled=True)  17.8 us
    dot_general x1, matrix products, on_device(): jnp.dot(scenario_draws, whole_of(cholesky, SCEN, (1, 0, 2), 0), preferred...  14.7 us
    dot_general x1, matrix products, on_device(): lax.dot_general(lax.all_gather(shocks, 'fac', axis=1, tiled=True), exposu...  14.7 us
    dot_general x1, matrix products, on_device(): lax.dot_general(gathered, pnl, (((0,), (0,)), ((), ())), preferred_elemen...  14.5 us
  transfers between devices with their start and end apart: 6, of which 6 were waited for; matrix products, arithmetic and copies ran while one was open for 1% of the time, Pallas kernels for 0%

profile of v1, /device:TPU:0, one launch (start us, length us, event | category | flops | bytes accessed | tf_op | source)
XLA Modules:
  0.0 542.7 jit_solution(4538596407335264963)
XLA Ops:
  7.2 0.0 all-gather.11.cloned.1.call-start
  7.2 10.6 %all-gather = bf16[256,1024]{1,0:T(8,128)(2,1)} all-gather(bf16[128,1024]{1,0:T(8,128)(2,1)} %param.5), channel_id=2, replica_groups=mesh['scen_0'=4,'scen_1'=2,'scen_2'=4,'fac'=4] {'scen_1'}, dimensions={0}, use_global_device_ids=true | all-gather | bytes 786432 | tf_op jit(solution)/shard_map/all_gather | solution.py:19
  17.8 0.0 all-gather.11.cloned.1.call-update
  17.8 0.0 all-gather.13.cloned.1.call-start
  17.9 33.2 %all-gather.11.cloned.1.call-done = bf16[8,128,1024]{2,1,0:T(8,128)(2,1)} async-done(((bf16[2,128,1024]{2,1,0:T(8,128)(2,1)}), bf16[8,128,1024]{2,1,0:T(8,128)(2,1)}) %all-gather.11.cloned.1.call-update) | async-done | bytes 2097168 | tf_op jit(solution)/shard_map/all_gather | solution.py:19
  51.1 0.0 all-gather.13.cloned.1.call-update
  51.1 0.0 all-gather.9.cloned.1.call-start
  51.2 84.5 %all-gather.13.cloned.1.call-done = bf16[16,2,128,1024]{3,2,1,0:T(8,128)(2,1)} async-done(((bf16[4,2,128,1024]{3,2,1,0:T(8,128)(2,1)}), bf16[16,2,128,1024]{3,2,1,0:T(8,128)(2,1)}) %all-gather.13.cloned.1.call-update) | async-done | bytes 8388624 | tf_op jit(solution)/shard_map/all_gather | solution.py:19
  135.7 0.0 copy-start.2
  135.7 8.2 %copy.13 = bf16[4,2,4,128,1024]{4,3,2,1,0:T(8,128)(2,1)} copy(bf16[4,2,4,128,1024]{4,3,1,0,2:T(8,128)(2,1)} %bitcast.22) | data formatting | bytes 16777216 | tf_op jit(solution)/shard_map/transpose | solution.py:22
  143.9 0.0 copy-done.2
  143.9 14.7 %add_convert_fusion = bf16[1024,1024]{1,0:T(8,128)(2,1)} fusion(f32[1024]{0:T(1024)S(1)} %copy-done.2, bf16[1024,4096]{1,0:T(8,128)(2,1)} %param.4, bf16[4096,1024]{1,0:T(8,128)(2,1)} %bitcast.24), kind=kOutput, calls=%fused_computation.1 | convolution fusion | flops 8592031744 | bytes 18878464 | tf_op jit(solution)/shard_map/dot_general | solution.py:42
  158.6 0.0 all-gather.9.cloned.1.call-update
  158.7 0.0 all-gather.15.cloned.1.call-start
  158.7 63.4 %all-gather.9.cloned.1.call-done = bf16[1024,4096]{1,0:T(8,128)(2,1)} async-done(((bf16[1024,1024]{1,0:T(8,128)(2,1)}), bf16[1024,4096]{1,0:T(8,128)(2,1)}) %all-gather.9.cloned.1.call-update) | async-done | bytes 8388624 | tf_op jit(solution)/shard_map/all_gather | solution.py:47
  222.1 14.7 %convolution_convert_fusion = bf16[1024,1024]{1,0:T(8,128)(2,1)} fusion(bf16[1024,4096]{1,0:T(8,128)(2,1)} %all-gather.9.cloned.1.call-done, bf16[1024,4096]{1,0:T(8,128)(2,1)} %param.6), kind=kOutput, calls=%fused_computation.2 | convolution fusion | flops 8590983168 | bytes 18874368 | tf_op jit(solution)/shard_map/dot_general | solution.py:46
  236.8 0.0 all-gather.15.cloned.1.call-update
  236.9 0.2 reduce-scatter.2.cloned.1.call-start
  237.1 61.6 %all-gather.15.cloned.1.call-done = bf16[4096,1024]{1,0:T(8,128)(2,1)} async-done(((bf16[1024,1024]{1,0:T(8,128)(2,1)}), bf16[4096,1024]{1,0:T(8,128)(2,1)}) %all-gather.15.cloned.1.call-update) | async-done | bytes 8388624 | tf_op jit(solution)/shard_map/all_gather | solution.py:53
  298.7 0.0 copy-start
  298.7 11.6 %copy.14 = bf16[4,1024,1024]{1,2,0:T(8,128)(2,1)} copy(bf16[4,1024,1024]{2,1,0:T(8,128)(2,1)} %bitcast.23) | data formatting | bytes 16777216 | tf_op jit(solution)/shard_map/all_gather | solution.py:53
  310.3 0.0 copy-done
  310.3 14.5 %fusion = f32[4096,1024]{1,0:T(8,128)} fusion(bf16[1024,4096]{0,1:T(8,128)(2,1)} %bitcast.21, bf16[1024,1024]{1,0:T(8,128)(2,1)S(1)} %copy-done), kind=kOutput, calls=%fused_computation.7 | convolution fusion | flops 8589934592 | bytes 27262976 | tf_op jit(solution)/shard_map/dot_general | solution.py:62
  324.8 0.0 reduce-scatter.2.cloned.1.call-update
  324.8 4.6 convert_reduce_fusion
  329.4 1.3 broadcast_in_dim.9
  330.7 7.3 %all-to-all-start = ((f32[32,1,4096]{2,1,0:T(1,128)}), f32[32,1,4096]{2,1,0:T(1,128)S(1)}, u32[]{:S(2)}, u32[]{:S(2)}) async-start(f32[32,1,4096]{2,1,0:T(1,128)} %broadcast_in_dim.9), calls=%async_computation.1 | async-start | bytes 1048576 | tf_op jit(solution)/shard_map/all_to_all | solution.py:32
  337.9 17.8 %all-to-all-done = f32[32,1,4096]{2,1,0:T(1,128)S(1)} async-done(((f32[32,1,4096]{2,1,0:T(1,128)}), f32[32,1,4096]{2,1,0:T(1,128)S(1)}, u32[]{:S(2)}, u32[]{:S(2)}) %all-to-all-start) | async-done | bytes 524320 | tf_op jit(solution)/shard_map/all_to_all | solution.py:32
  355.7 0.4 reduce_sum.19
  356.1 0.0 copy-start.1
  356.1 0.1 dynamic-slice_multiply_fusion
  356.2 178.0 %reduce-scatter.2.cloned.1.call-done = f32[128,1024]{1,0:T(8,128)} async-done(((f32[4096,1024]{1,0:T(8,128)}), f32[128,1024]{1,0:T(8,128)}) %reduce-scatter.2.cloned.1.call-update) | async-done | bytes 524304 | tf_op jit(solution)/shard_map/reduce_scatter | solution.py:61
  534.2 2.0 subtract_multiply_fusion
  536.1 0.0 copy-done.1
  (3 shorter events, 0.0 us)
Async XLA Ops:
  7.2 43.9 %all-gather.11.cloned.1.call-start = ((), (), s32[]{:S(2)}) async-start(), calls=%async_computation.4 | async-start | bytes 2621440 | tf_op jit(solution)/shard_map/all_gather | solution.py:19
  17.8 117.8 %all-gather.13.cloned.1.call-start = ((), (), s32[]{:S(2)}) async-start(), calls=%async_computation.5 | async-start | bytes 10485760 | tf_op jit(solution)/shard_map/all_gather | solution.py:19
  51.1 171.0 %all-gather.9.cloned.1.call-start = ((), (), s32[]{:S(2)}) async-start(), calls=%async_computation.2 | async-start | bytes 10485760 | tf_op jit(solution)/shard_map/all_gather | solution.py:47
  135.7 8.2 %copy-start.2 = (f32[1024]{0:T(1024)S(1)}, f32[1024]{0:T(1024)}, u32[]{:S(2)}) copy-start(f32[1024]{0:T(1024)} %param.7) | copy-start | bytes 12292
  158.7 140.1 %all-gather.15.cloned.1.call-start = ((), (), s32[]{:S(2)}) async-start(), calls=%async_computation.6 | async-start | bytes 10485760 | tf_op jit(solution)/shard_map/all_gather | solution.py:53
  236.9 297.3 %reduce-scatter.2.cloned.1.call-start = ((), (), s32[]{:S(2)}) async-start(), calls=%async_computation.3 | async-start | bytes 17301504 | tf_op jit(solution)/shard_map/reduce_scatter | solution.py:61
  298.7 11.6 %copy-start = (bf16[1024,1024]{1,0:T(8,128)(2,1)S(1)}, bf16[1024,1024]{1,0:T(8,128)(2,1)}, u32[]{:S(2)}) copy-start(bf16[1024,1024]{1,0:T(8,128)(2,1)} %convolution_convert_fusion) | copy-start | bytes 6291460
  330.7 25.1 %all-to-all-start = ((f32[32,1,4096]{2,1,0:T(1,128)}), f32[32,1,4096]{2,1,0:T(1,128)S(1)}, u32[]{:S(2)}, u32[]{:S(2)}) async-start(f32[32,1,4096]{2,1,0:T(1,128)} %broadcast_in_dim.9), calls=%async_computation.1 | async-start | bytes 1048576 | tf_op jit(solution)/shard_map/all_to_all | solution.py:32
  356.1 180.0 %copy-start.1 = (f32[1024]{0:T(1024)}, f32[1024]{0:T(1024)S(1)}, u32[]{:S(2)}) copy-start(f32[1024]{0:T(1024)S(1)} %dynamic_slice.7) | copy-start | bytes 12292
Sparse Core Ops, SparseCore 0:
  18.0 33.0 all-gather.10
  52.7 82.8 all-gather.12
  158.8 63.2 all-gather.8
  237.0 61.7 all-gather.14
  325.0 209.1 reduce-scatter.1
